TPU v7x, 32 devices: a whole 2x2x4 slice. The times are simulated.
32 devices in a mesh: hx: 4 (over y, x), hy: 4 (over z), tok: 2 (over core).
Axes of the slice: x: 2, y: 2, z: 4, core: 2. Of those that a mesh axis runs over, the one named last changes fastest.
Arguments:
- stream_in: bfloat16 [512, 4608], P('tok', ('hx', 'hy')), may hold values from -6 to 6
- before_gain: bfloat16 [4608], P(('hx', 'hy')), may hold values from 0.25 to 1.75
- after_gain: bfloat16 [4608], P(('hx', 'hy')), may hold values from 0.25 to 1.75
- feed_gain: bfloat16 [4608], P(('hx', 'hy')), may hold values from 0.25 to 1.75
- query_weight: bfloat16 [4608, 4096], P('tok', ('hx', 'hy')), may hold values from -1 to 1
- key_weight: bfloat16 [4608, 2048], P('tok', ('hx', 'hy')), may hold values from -64 to 64
- value_weight: bfloat16 [4608, 2048], P('tok', ('hx', 'hy')), may hold values from -0.09375 to 0.09375
- output_weight: bfloat16 [4096, 4608], P(('hx', 'hy'), 'tok'), may hold values from -0.09375 to 0.09375
- documents: int32 [512], P('tok'), may hold values from 0 to 7, never falling along the last dimension, each value on 1 to 128 neighbouring positions
Outputs:
- residual: bfloat16 [512, 4608], P('tok', ('hx', 'hy'))
- feed_input: bfloat16 [512, 4608], P('tok', ('hx', 'hy'))
Inputs may be any that keep to these rules, and one draw needn't show every extreme that they name: `documents`: ids never fall along the tokens; a document holds at most 128 tokens and may run across a sequence's end.
All inputs are finite; a program needn't handle non-finite values.
Results may differ from a plain program's by a relative error of at most 0.014.
The roundings to bfloat16 on the way count: a program that leaves them out, or rounds other values in their place, can miss the bound.
Values may be sent and summed in bfloat16 or wider, within the bound.
A program may use at most 64 MiB of HBM per device.

v0:
```python
import jax
import jax.numpy as jnp
from jax import lax
from jax.sharding import PartitionSpec as P

D = 4608
QH = 32
HEAD = 128
LENGTH = 256


epsilon = 1e-06
neg_big = -1e30


def rotate(values, positions):
    half_width = values.shape[-1] // 2
    frequency = 10000.0 ** (-jnp.arange(half_width, dtype=jnp.float32) / half_width)
    angles = positions.astype(jnp.float32)[:, None] * frequency[None, :]
    cosine_table = jnp.cos(angles)[:, None, :]
    sine_table = jnp.sin(angles)[:, None, :]
    leading = values[..., :half_width]
    trailing = values[..., half_width:]
    return jnp.concatenate(
        [
            leading * cosine_table - trailing * sine_table,
            trailing * cosine_table + leading * sine_table,
        ],
        axis=-1,
    )


def per_device(
    stream_in,
    before_gain,
    after_gain,
    feed_gain,
    query_weight,
    key_weight,
    value_weight,
    output_weight,
    documents,
):
    rows = stream_in.shape[0]
    wide = stream_in.astype(jnp.float32)
    first_sq = lax.psum(jnp.sum(wide * wide, axis=1), ("hx", "hy"))
    first_scale = lax.rsqrt(first_sq / D + epsilon)
    normed_local = (wide * first_scale[:, None] * before_gain.astype(jnp.float32)[None, :]).astype(
        jnp.bfloat16
    )
    normed = lax.all_gather(normed_local, ("hx", "hy"), axis=1, tiled=True)
    pieces = (
        lax.all_gather(query_weight, "tok", axis=0, tiled=True),
        lax.all_gather(key_weight, "tok", axis=0, tiled=True),
        lax.all_gather(value_weight, "tok", axis=0, tiled=True),
    )
    query_sum, key_sum, value_sum = tuple(
        (jnp.dot(normed, piece, preferred_element_type=jnp.float32) for piece in pieces)
    )
    query_heads = query_weight.shape[1] // HEAD
    key_heads = key_weight.shape[1] // HEAD
    ratio = query_heads // key_heads
    positions = jnp.arange(rows, dtype=jnp.int32) % LENGTH
    count_seq = rows // LENGTH
    queries = (
        (rotate(query_sum.reshape(rows, query_heads, HEAD), positions) * (D / QH) ** (-0.5))
        .astype(jnp.bfloat16)
        .reshape(count_seq, LENGTH, key_heads, ratio, HEAD)
    )
    keys = (
        rotate(key_sum.reshape(rows, key_heads, HEAD), positions)
        .astype(jnp.bfloat16)
        .reshape(count_seq, LENGTH, key_heads, HEAD)
    )
    values = value_sum.astype(jnp.bfloat16).reshape(count_seq, LENGTH, key_heads, HEAD)
    doc_seq = documents.reshape(count_seq, LENGTH)

    def one_sequence(items):
        query_part, key_part, value_part, doc_part = items
        scores = jnp.einsum(
            "tkrh,skh->tkrs", query_part, key_part, preferred_element_type=jnp.float32
        )
        index = jnp.arange(LENGTH)
        allowed = (index[None, :] <= index[:, None]) & (doc_part[None, :] == doc_part[:, None])
        mask = allowed[:, None, None, :]
        best = jnp.max(jnp.where(mask, scores, neg_big), axis=-1, keepdims=True)
        weights = jnp.where(mask, jnp.exp(scores - best), 0.0)
        total = jnp.sum(weights, axis=-1)
        summed = jnp.einsum(
            "tkrs,skh->tkrh",
            weights.astype(jnp.bfloat16),
            value_part,
            preferred_element_type=jnp.float32,
        )
        return (summed / total[..., None]).astype(jnp.bfloat16)

    attended = lax.map(one_sequence, (queries, keys, values, doc_seq)).reshape(
        rows, query_heads * HEAD
    )
    terms = jnp.dot(
        attended,
        lax.all_gather(output_weight, "tok", axis=1, tiled=True),
        preferred_element_type=jnp.float32,
    )
    mixed = lax.psum_scatter(
        terms.astype(jnp.bfloat16), ("hx", "hy"), scatter_dimension=1, tiled=True
    ).astype(jnp.float32)
    gain_after = after_gain.astype(jnp.float32)[None, :]
    gain_feed = feed_gain.astype(jnp.float32)[None, :]
    branch = mixed * gain_after
    after_sq, cross_sum, branch_sq = lax.psum(
        (
            jnp.sum(mixed * mixed, axis=1),
            jnp.sum(wide * branch, axis=1),
            jnp.sum(branch * branch, axis=1),
        ),
        ("hx", "hy"),
    )
    after_scale = lax.rsqrt(after_sq / D + epsilon)
    residual = (wide + mixed * after_scale[:, None] * gain_after).astype(jnp.bfloat16)
    residual_wide = residual.astype(jnp.float32)
    feed_sq = first_sq + 2.0 * after_scale * cross_sum + after_scale * after_scale * branch_sq
    feed_scale = lax.rsqrt(feed_sq / D + epsilon)
    feed_input = (residual_wide * feed_scale[:, None] * gain_feed).astype(jnp.bfloat16)
    return (residual, feed_input)


def solution(mesh):
    in_specs = (
        P("tok", ("hx", "hy")),
        P(("hx", "hy")),
        P(("hx", "hy")),
        P(("hx", "hy")),
        P("tok", ("hx", "hy")),
        P("tok", ("hx", "hy")),
        P("tok", ("hx", "hy")),
        P(("hx", "hy"), "tok"),
        P("tok"),
    )
    out_specs = (P("tok", ("hx", "hy")), P("tok", ("hx", "hy")))
    return jax.shard_map(
        per_device, mesh=mesh, in_specs=in_specs, out_specs=out_specs, check_vma=False
    )
```

profile of v0, /device:TPU:0, one launch (start us, length us, event | category | flops | bytes accessed | tf_op | source)
XLA Modules:
  0.0 333.1 jit_solution(18040886991750297897)
XLA Ops:
  7.2 0.7 all-gather.12.cloned.1.call-update
  8.0 0.7 convert_element_type.78
  8.6 1.0 fusion.9
  9.6 43.7 %psum.28 = f32[256]{0:T(256)S(1)} all-reduce(f32[256]{0:T(256)S(1)} %fusion.9), channel_id=1, replica_groups=mesh['hx'=4,'hy'=4,'tok'=2] {'hx','hy'}, use_global_device_ids=true, to_apply=%region_1.0 | all-reduce | flops 256 | bytes 2048 | tf_op jit(solution)/shard_map/psum | solution.py:46
  53.4 1.7 fusion.11
  55.1 0.7 all-gather.10.cloned.1.call-update
  55.8 0.5 all-gather.8.cloned.1.call-update
  56.4 0.5 all-gather.14.cloned.1.call-update
  57.2 0.5 multiply_cosine_fusion
  57.7 56.0 %all-gather.6.cloned.1.call-done = bf16[256,4608]{0,1:T(8,128)(2,1)} async-done(((bf16[256,288]{0,1:T(8,128)(2,1)}), bf16[256,4608]{0,1:T(8,128)(2,1)}) %all-gather.6.cloned.1.call-update) | async-done | bytes 2359312 | tf_op jit(solution)/shard_map/all_gather | solution.py:51
  113.7 3.6 %fusion.42 = f32[256,256]{0,1:T(8,128)S(1)} fusion(bf16[256,4608]{0,1:T(8,128)(2,1)} %all-gather.6.cloned.1.call-done, bf16[4608,256]{1,0:T(8,128)(2,1)} %all-gather.12.cloned.1.call-done), kind=kOutput, calls=%fused_computation.68 | convolution fusion | flops 603979776 | bytes 4980736 | tf_op jit(solution)/shard_map/dot_general | solution.py:58
  117.5 5.3 %all-gather.10.cloned.1.call-done = bf16[4608,128]{1,0:T(8,128)(2,1)} async-done(((bf16[2304,128]{1,0:T(8,128)(2,1)}), bf16[4608,128]{1,0:T(8,128)(2,1)}) %all-gather.10.cloned.1.call-update) | async-done | bytes 1179664 | tf_op jit(solution)/shard_map/all_gather | solution.py:54
  122.8 1.9 convolution_bitcast_fusion.2
  124.8 0.3 fusion.34
  125.2 0.4 select_reduce_fusion
  125.7 9.0 %all-gather.8.cloned.1.call-done = bf16[4608,128]{1,0:T(8,128)(2,1)} async-done(((bf16[2304,128]{1,0:T(8,128)(2,1)}), bf16[4608,128]{1,0:T(8,128)(2,1)}) %all-gather.8.cloned.1.call-update) | async-done | bytes 1179664 | tf_op jit(solution)/shard_map/all_gather | solution.py:55
  134.7 2.0 fusion.2
  136.7 11.5 %all-gather.14.cloned.1.call-done = bf16[256,4608]{1,0:T(8,128)(2,1)} async-done(((bf16[256,2304]{1,0:T(8,128)(2,1)}), bf16[256,4608]{1,0:T(8,128)(2,1)}) %all-gather.14.cloned.1.call-update) | async-done | bytes 2359312 | tf_op jit(solution)/shard_map/all_gather | solution.py:102
  148.2 4.1 %convolution_convert_fusion = bf16[256,4608]{0,1:T(8,128)(2,1)} fusion(bf16[256,256]{0,1:T(8,128)(2,1)S(1)} %bitcast.41, bf16[256,4608]{1,0:T(8,128)(2,1)} %all-gather.14.cloned.1.call-done), kind=kOutput, calls=%fused_computation | convolution fusion | flops 605159424 | bytes 4849664 | tf_op jit(solution)/shard_map/dot_general | solution.py:100
  152.4 0.6 copy-done.2
  153.1 130.4 %reduce-scatter.2.cloned.1.call-done = bf16[256,288]{0,1:T(8,128)(2,1)} async-done(((bf16[256,4608]{0,1:T(8,128)(2,1)}), bf16[256,288]{0,1:T(8,128)(2,1)}) %reduce-scatter.2.cloned.1.call-update) | async-done | bytes 147472 | tf_op jit(solution)/shard_map/reduce_scatter | solution.py:105
  283.5 1.0 fusion.13
  284.5 40.0 %all-reduce = (f32[256]{0:T(256)S(1)}, f32[256]{0:T(256)S(1)}, f32[256]{0:T(256)S(1)}) all-reduce(f32[256]{0:T(256)S(1)} %get-tuple-element.16, f32[256]{0:T(256)S(1)} %get-tuple-element.15, f32[256]{0:T(256)S(1)} %get-tuple-element.14), channel_id=1, replica_groups=mesh['hx'=4,'hy'=4,'tok'=2] {'hx','hy'}, use_global_device_ids=true, to_apply=%region_6.7 | all-reduce | flops 768 | bytes 6144 | tf_op jit(solution)/shard_map/psum | solution.py:111
  324.5 1.8 multiply_convert_fusion
  (30 shorter events, 0.9 us)
Async XLA Ops:
  7.2 49.8 %copy-start.1 = (s32[256]{0:T(256)S(1)}, s32[256]{0:T(256)}, u32[]{:S(2)}) copy-start(s32[256]{0:T(256)} %param.17) | copy-start | bytes 3076
  7.2 50.5 %all-gather.12.cloned.1.call-start = ((), (), s32[]{:S(2)}) async-start(), calls=%async_computation.4 | async-start | bytes 3538944 | tf_op jit(solution)/shard_map/all_gather | solution.py:53
  7.9 105.8 %all-gather.6.cloned.1.call-start = ((), (), s32[]{:S(2)}) async-start(), calls=%async_computation.1 | async-start | bytes 2506752 | tf_op jit(solution)/shard_map/all_gather | solution.py:51
  55.1 67.8 %all-gather.10.cloned.1.call-start = ((), (), s32[]{:S(2)}) async-start(), calls=%async_computation.3 | async-start | bytes 1769472 | tf_op jit(solution)/shard_map/all_gather | solution.py:54
  55.8 78.9 %all-gather.8.cloned.1.call-start = ((), (), s32[]{:S(2)}) async-start(), calls=%async_computation.2 | async-start | bytes 1769472 | tf_op jit(solution)/shard_map/all_gather | solution.py:55
  56.4 91.9 %all-gather.14.cloned.1.call-start = ((), (), s32[]{:S(2)}) async-start(), calls=%async_computation.5 | async-start | bytes 3538944 | tf_op jit(solution)/shard_map/all_gather | solution.py:102
  57.0 226.5 %reduce-scatter.2.cloned.1.call-start = ((), (), s32[]{:S(2)}) async-start(), calls=%async_computation.6 | async-start | bytes 2506752 | tf_op jit(solution)/shard_map/reduce_scatter | solution.py:105
  113.7 9.2 %copy-start.4 = (bf16[256,4608]{0,1:T(8,128)(2,1)S(1)}, bf16[256,4608]{0,1:T(8,128)(2,1)}, u32[]{:S(2)}) copy-start(bf16[256,4608]{0,1:T(8,128)(2,1)} %all-gather.6.cloned.1.call-done) | copy-start | bytes 7077892
  152.4 0.7 copy-start.2
  152.4 0.7 copy-start.3
  152.4 131.1 %copy-start = (bf16[256,288]{0,1:T(8,128)(2,1)S(1)}, bf16[256,288]{0,1:T(8,128)(2,1)}, u32[]{:S(2)}) copy-start(bf16[256,288]{0,1:T(8,128)(2,1)} %param.9) | copy-start | bytes 442372
Sparse Core Ops, SparseCore 0:
  9.5 13.6 all-gather.11
  55.2 58.4 all-gather.5
  115.2 7.5 all-gather.9
  124.2 10.3 all-gather.7
  136.1 12.1 all-gather.13
  153.0 130.4 reduce-scatter.1
where the time goes:
time: 333 us
  waiting for transfers between devices  215 us (65%)
  blocking collectives  83.7 us (25%)
  between operations  14.2 us (4%)
  matrix products  12 us (4%)
  other arithmetic  7.35 us (2%)
    reduce_scatter x1, waiting for transfers between devices, per_device(): lax.psum_scatter(terms.astype(jnp.bfloat16), ('hx', 'hy'), scatter_dimens...  130 us
    all_gather x1, waiting for transfers between devices, per_device(): normed = lax.all_gather(normed_local, ('hx', 'hy'), axis=1, tiled=True)  56 us
    psum x1, blocking collectives, per_device(): first_sq = lax.psum(jnp.sum(wide * wide, axis=1), ('hx', 'hy'))  43.7 us
    psum x1, blocking collectives, per_device(): lax.psum((jnp.sum(mixed * mixed, axis=1), jnp.sum(wide * branch, axis=1),...  40 us
    all_gather x1, waiting for transfers between devices, per_device(): lax.all_gather(output_weight, 'tok', axis=1, tiled=True)  11.5 us
    all_gather x1, waiting for transfers between devices, per_device(): lax.all_gather(value_weight, 'tok', axis=0, tiled=True)  9 us
  transfers between devices with their start and end apart: 6, of which 5 were waited for; matrix products, arithmetic and copies ran while one was open for 4% of the time, Pallas kernels for 0%

commit v1 on v0

v1 whole, which is shorter than its diff:
```python
import functools

import jax
import jax.numpy as jnp
import numpy as np
from jax import lax
from jax.experimental import pallas as pl
from jax.experimental.pallas import tpu as pltpu
from jax.sharding import PartitionSpec as P

D = 4608
QH = 32
HEAD = 128
LENGTH = 256
LANES = 128

epsilon = 1e-06
neg_big = -1e30
MESH = pl.DeviceIdType.MESH
F32 = jnp.float32
BF16 = jnp.bfloat16


def flip(index, mask):
    low = (index % 2 + mask % 2) % 2
    high = (index // 2 + mask // 2) % 2
    return low + 2 * high


def rope_tables():
    half = HEAD // 2
    frequency = (10000.0 ** (-np.arange(half, dtype=np.float32) / half)).astype(np.float32)
    angles = np.arange(LENGTH, dtype=np.float32)[:, None] * frequency[None, :]
    cosine, sine = np.cos(angles), np.sin(angles)
    table = np.stack([np.concatenate([cosine, cosine], 1), np.concatenate([-sine, sine], 1)])
    return table.astype(np.float32)


def kernel(
    paired,
    stream, gains, docs, tables, wq, wk, wv, wo,
    residual_out, feed_out,
    raw, slots, docs_v, tables_v, weights, out_weight, out_main, out_tail,
    terms, first_a, first_b, from_x, from_y, from_z, stats, stats_in, stats_mid, stats_zin,
    local_sem, weight_send, weight_recv, gather_send, gather_recv, reduce_send, reduce_recv,
    stat_send, stat_recv,
):
    rows, width = raw.shape
    full, rest = width // LANES, width % LANES
    per = LANES // rest
    tail_rows = rows // per
    body = full * rows
    size = body + tail_rows
    a, b, c = lax.axis_index("hx"), lax.axis_index("hy"), lax.axis_index("tok")
    along_x, along_y, across = flip(a, 1), flip(a, 2), flip(a, 3)
    z_peers = [None] + [flip(b, j) for j in (1, 2, 3)]

    def group_of(i, j):
        return flip(a, i) * 4 + flip(b, j)

    locals_ = [
        pltpu.make_async_copy(stream, raw, local_sem.at[0]),
        pltpu.make_async_copy(gains, slots.at[0, pl.ds(size, 16)], local_sem.at[1]),
        pltpu.make_async_copy(docs, docs_v, local_sem.at[2]),
        pltpu.make_async_copy(tables, tables_v, local_sem.at[3]),
    ]
    for copy in locals_:
        copy.start()
    wrows, qcols, kcols = wq.shape[0], wq.shape[1], wk.shape[1]
    shard = c if paired else 0
    start = pl.multiple_of(shard * wrows, 16)
    targets = [
        (wo, out_weight.at[shard]),
        (wq, weights.at[pl.ds(start, wrows), pl.ds(0, qcols)]),
        (wk, weights.at[pl.ds(start, wrows), pl.ds(qcols, kcols)]),
        (wv, weights.at[pl.ds(start, wrows), pl.ds(qcols + kcols, kcols)]),
    ]
    weight_local = [
        pltpu.make_async_copy(src, dst, local_sem.at[4 + k]) for k, (src, dst) in enumerate(targets)
    ]

    barrier = pltpu.get_barrier_semaphore()
    greet = [{"hx": along_x}, {"hx": along_y}, {"hx": across}]
    greet += [{"hy": z_peers[j]} for j in (1, 2, 3)]
    if paired:
        greet.append({"tok": 1 - c})
    for peer in greet:
        pl.semaphore_signal(barrier, inc=1, device_id=peer, device_id_type=MESH)
    for copy in weight_local:
        copy.start()

    lane = lax.broadcasted_iota(jnp.int32, (tail_rows, LANES), 1)
    locals_[0].wait()
    for k in range(full):
        slots[0, k * rows:(k + 1) * rows, :] = raw[:, k * LANES:(k + 1) * LANES]
    tail = raw[:, full * LANES:width].astype(F32)
    packed = jnp.concatenate(
        [tail[r * tail_rows:(r + 1) * tail_rows] for r in range(per)], axis=1
    )
    slots[0, body:size, :] = packed.astype(BF16)
    locals_[1].wait()
    pl.semaphore_wait(barrier, len(greet))

    def remote(src, dst, send, recv, peer):
        return pltpu.make_async_remote_copy(
            src_ref=src, dst_ref=dst, send_sem=send, recv_sem=recv, device_id=peer, device_id_type=MESH
        )

    total_rows = size + 16
    cut = (total_rows // 32) * 16

    def gather_z(j):
        return remote(slots.at[0], slots.at[j], gather_send.at[j], gather_recv.at[j], {"hy": z_peers[j]})

    def gather_x(j):
        return remote(slots.at[j], slots.at[4 + j], gather_send.at[4 + j], gather_recv.at[4 + j], {"hx": along_x})

    def gather_y(j):
        return remote(slots.at[j], slots.at[8 + j], gather_send.at[8 + j], gather_recv.at[8 + j], {"hx": along_y})

    def relay_a(j):
        part = pl.ds(0, cut)
        return remote(
            slots.at[4 + j, part], slots.at[12 + j, part], gather_send.at[12 + j], gather_recv.at[12 + j], {"hx": along_y}
        )

    def relay_b(j):
        part = pl.ds(cut, total_rows - cut)
        return remote(
            slots.at[8 + j, part], slots.at[12 + j, part], gather_send.at[16 + j], gather_recv.at[16 + j], {"hx": along_x}
        )

    gather_x(0).start()
    gather_y(0).start()
    for j in (1, 2, 3):
        gather_z(j).start()
    weight_remote = []
    if paired:
        weight_remote = [
            remote(src, dst, weight_send.at[k], weight_recv.at[k], {"tok": 1 - c})
            for k, (src, dst) in enumerate(targets)
        ]
        for copy in weight_remote:
            copy.start()

    def forward(j):
        gather_z(j).wait_recv()
        gather_x(j).start()
        gather_y(j).start()

    def relay(j):
        gather_x(j).wait_recv()
        relay_a(j).start()
        gather_y(j).wait_recv()
        relay_b(j).start()

    shards = out_weight.shape[0]
    per_shard = 16 // shards

    def prepare_out(g):
        offset = (g % per_shard) * width
        base = offset // LANES * LANES
        shift = offset - base
        span = (full + 1) * LANES
        piece = out_weight[g // per_shard, :, base:base + span].astype(F32)
        if shift:
            piece = pltpu.roll(piece, span - shift, 1)
        piece = piece.astype(BF16)
        out_main[g] = piece[:, :full * LANES]
        return piece[:, full * LANES:].astype(F32)

    def prepare_outs(q):
        wide_lane = lax.broadcasted_iota(jnp.int32, (out_weight.shape[1], LANES), 1)
        held = None
        for r in range(per):
            part = prepare_out(q * per + r)
            if r:
                part = pltpu.roll(part, r * rest, 1)
            held = part if r == 0 else jnp.where(wide_lane // rest == r, part, held)
        out_tail[:, q * LANES:(q + 1) * LANES] = held.astype(BF16)

    forward(1)
    relay(0)
    weight_local[0].wait()
    if paired:
        weight_remote[0].wait_recv()
    prepare_outs(0)
    forward(2)
    relay(1)
    prepare_outs(1)
    forward(3)
    relay(2)
    prepare_outs(2)
    prepare_outs(3)
    locals_[2].wait()
    locals_[3].wait()
    doc_col = jnp.concatenate([docs_v[...]] * (LANES // 8), axis=0).T[:, 0:1]
    doc_row = docs_v[0:1, :]
    t_index = lax.broadcasted_iota(jnp.int32, (LENGTH, LENGTH), 0)
    s_index = lax.broadcasted_iota(jnp.int32, (LENGTH, LENGTH), 1)
    for copy in weight_local[1:]:
        copy.wait()
    if paired:
        for copy in weight_remote[1:]:
            copy.wait_recv()
    relay(3)
    for j in range(4):
        relay_a(j).wait_recv()
        relay_b(j).wait_recv()

    def tails_of(i):
        out = []
        for r in range(per):
            held = None
            for j in range(per):
                part = slots[4 * i + j, body:size, :].astype(F32)
                move = (rest * (j - r)) % LANES
                if move:
                    part = pltpu.roll(part, move, 1)
                held = part if j == 0 else jnp.where(lane // rest == j, part, held)
            out.append(held)
        return jnp.concatenate(out, axis=0)

    squares = jnp.zeros((rows, LANES), F32)
    tails = []
    for i in range(4):
        for j in range(4):
            for k in range(full):
                part = slots[4 * i + j, k * rows:(k + 1) * rows, :].astype(F32)
                squares = squares + part * part
        unpacked = tails_of(i)
        tails.append(unpacked)
        squares = squares + unpacked * unpacked
    first_sq = jnp.sum(squares, axis=1, keepdims=True)
    first_scale = lax.rsqrt(first_sq / D + epsilon)
    sums = None
    lane_row = lax.broadcasted_iota(jnp.int32, (1, LANES), 1)
    for i in range(4):
        columns, w_main, w_tail = [], [], []
        tail_gain = None
        for j in range(4):
            gain = slots[4 * i + j, size:size + 16, :].astype(F32)
            for k in range(full):
                part = slots[4 * i + j, k * rows:(k + 1) * rows, :].astype(F32)
                columns.append((part * first_scale * gain[k:k + 1]).astype(BF16))
            last = gain[full:full + 1]
            tail_gain = last if j == 0 else jnp.where(lane_row // rest == j, last, tail_gain)
            at = group_of(i, j) * width
            w_main.append(weights[pl.ds(pl.multiple_of(at, 16), full * LANES), :])
            w_tail.append(weights[pl.ds(pl.multiple_of(at + full * LANES, 16), rest), :])
        columns.append((tails[i] * first_scale * tail_gain).astype(BF16))
        part = jnp.dot(
            jnp.concatenate(columns, axis=1), jnp.concatenate(w_main + w_tail, axis=0), preferred_element_type=F32
        )
        sums = part if sums is None else sums + part

    cosine, sine = tables_v[0], tables_v[1]

    def rope(x):
        return x * cosine + pltpu.roll(x, HEAD // 2, 1) * sine

    query_heads, key_heads = qcols // HEAD, kcols // HEAD
    ratio = query_heads // key_heads
    allowed = (s_index <= t_index) & (doc_row == doc_col)
    attended = []
    for h in range(query_heads):
        kv = h // ratio
        query = (rope(sums[:, h * HEAD:(h + 1) * HEAD]) * (D / QH) ** (-0.5)).astype(BF16)
        key = rope(sums[:, qcols + kv * HEAD:qcols + (kv + 1) * HEAD]).astype(BF16)
        value = sums[:, qcols + kcols + kv * HEAD:qcols + kcols + (kv + 1) * HEAD].astype(BF16)
        scores = lax.dot_general(query, key, (((1,), (1,)), ((), ())), preferred_element_type=F32)
        best = jnp.max(jnp.where(allowed, scores, neg_big), axis=1, keepdims=True)
        soft = jnp.where(allowed, jnp.exp(scores - best), 0.0)
        total = jnp.sum(soft, axis=1, keepdims=True)
        mixed_values = jnp.dot(soft.astype(BF16), value, preferred_element_type=F32)
        attended.append((mixed_values / total).astype(BF16))
    attended = jnp.concatenate(attended, axis=1)

    for q in range(4):
        tail_terms = jnp.dot(attended, out_tail[:, q * LANES:(q + 1) * LANES], preferred_element_type=F32)
        for r in range(per):
            g = q * per + r
            main = jnp.dot(attended, out_main[g], preferred_element_type=F32).astype(BF16)
            for k in range(full):
                terms[g, k * rows:(k + 1) * rows, :] = main[:, k * LANES:(k + 1) * LANES]
            held = None
            for s in range(per):
                part = tail_terms[s * tail_rows:(s + 1) * tail_rows]
                move = (rest * (s - r)) % LANES
                if move:
                    part = pltpu.roll(part, move, 1)
                held = part if s == 0 else jnp.where(lane // rest == s, part, held)
            terms[g, body:size, :] = held.astype(BF16)

    half = size // 2
    top, bottom = pl.ds(0, half), pl.ds(half, half)

    def diagonal_a(j):
        return remote(
            terms.at[group_of(3, j), top], first_a.at[j], reduce_send.at[j], reduce_recv.at[j], {"hx": along_x}
        )

    def diagonal_b(j):
        return remote(
            terms.at[group_of(3, j), bottom], first_b.at[j], reduce_send.at[4 + j], reduce_recv.at[4 + j], {"hx": along_y}
        )

    def reduce_x(j):
        return remote(
            terms.at[group_of(1, j)], from_x.at[j], reduce_send.at[8 + j], reduce_recv.at[8 + j], {"hx": along_x}
        )

    def reduce_y(j):
        return remote(
            terms.at[group_of(2, j)], from_y.at[j], reduce_send.at[12 + j], reduce_recv.at[12 + j], {"hx": along_y}
        )

    def reduce_z(j):
        return remote(
            terms.at[group_of(0, j)], from_z.at[j - 1], reduce_send.at[15 + j], reduce_recv.at[15 + j], {"hy": z_peers[j]}
        )

    order = (3, 2, 1, 0)
    for j in order:
        diagonal_a(j).start()
        diagonal_b(j).start()

    def second(j):
        diagonal_a(j).wait_recv()
        g = group_of(2, j)
        terms[g, top, :] = (terms[g, top, :].astype(F32) + first_a[j].astype(F32)).astype(BF16)
        reduce_y(j).start()
        diagonal_b(j).wait_recv()
        g = group_of(1, j)
        terms[g, bottom, :] = (terms[g, bottom, :].astype(F32) + first_b[j].astype(F32)).astype(BF16)
        reduce_x(j).start()

    def plane_sum(j):
        reduce_x(j).wait_recv()
        reduce_y(j).wait_recv()
        return terms[group_of(0, j)].astype(F32) + from_x[j].astype(F32) + from_y[j].astype(F32)

    for j in order:
        second(j)
    for j in (3, 2, 1):
        terms[group_of(0, j)] = plane_sum(j).astype(BF16)
        reduce_z(j).start()
    mixed = plane_sum(0)
    for j in (3, 2, 1):
        reduce_z(j).wait_recv()
        mixed = mixed + from_z[j - 1].astype(F32)

    gain = slots[0, size:size + 16, :].astype(F32)
    pieces = [mixed[k * rows:(k + 1) * rows] for k in range(full)]
    last = []
    for r in range(per):
        part = mixed[body:size]
        if r:
            part = pltpu.roll(part, LANES - r * rest, 1)
        last.append(jnp.where(lane < rest, part, 0.0))
    pieces.append(jnp.concatenate(last, axis=0))
    wides = [raw[:, k * LANES:(k + 1) * LANES].astype(F32) for k in range(full)]
    own = tails[0]
    padded = jnp.concatenate([raw[:, full * LANES:width].astype(F32), jnp.zeros((rows, LANES - rest), F32)], axis=1)
    wides.append(padded)
    squares = cross = branch_sq = jnp.zeros((rows, LANES), F32)
    for k in range(full + 1):
        branch = pieces[k] * gain[full + 1 + k:full + 2 + k]
        squares = squares + pieces[k] * pieces[k]
        cross = cross + wides[k] * branch
        branch_sq = branch_sq + branch * branch
    all_lane = lax.broadcasted_iota(jnp.int32, (rows, LANES), 1)
    three = jnp.where(
        all_lane == 0,
        jnp.sum(squares, axis=1, keepdims=True),
        jnp.where(
            all_lane == 1,
            jnp.sum(cross, axis=1, keepdims=True),
            jnp.sum(branch_sq, axis=1, keepdims=True),
        ),
    )
    stats[...] = three.T[0:8]
    plane = (None, along_x, along_y, across)

    def stat_plane(i):
        return remote(stats, stats_in.at[i - 1], stat_send.at[i - 1], stat_recv.at[i - 1], {"hx": plane[i]})

    def stat_z(j):
        return remote(stats_mid, stats_zin.at[j - 1], stat_send.at[2 + j], stat_recv.at[2 + j], {"hy": z_peers[j]})

    for i in (3, 2, 1):
        stat_plane(i).start()
    for i in (1, 2, 3):
        stat_plane(i).wait_recv()
    stats_mid[...] = stats[...] + stats_in[0] + stats_in[1] + stats_in[2]
    for j in (3, 2, 1):
        stat_z(j).start()
    for j in (1, 2, 3):
        stat_z(j).wait_recv()
    summed = stats_mid[...] + stats_zin[0] + stats_zin[1] + stats_zin[2]
    back = jnp.concatenate([summed] * (LANES // 8), axis=0).T
    after_sq, cross_sum, branch_sum = back[:, 0:1], back[:, 1:2], back[:, 2:3]
    after_scale = lax.rsqrt(after_sq / D + epsilon)
    feed_sq = first_sq + 2.0 * after_scale * cross_sum + after_scale * after_scale * branch_sum
    feed_scale = lax.rsqrt(feed_sq / D + epsilon)
    for k in range(full + 1):
        n = LANES if k < full else rest
        residual = (wides[k] + pieces[k] * after_scale * gain[full + 1 + k:full + 2 + k]).astype(BF16)
        feed = (residual.astype(F32) * feed_scale * gain[2 * full + 2 + k:2 * full + 3 + k]).astype(BF16)
        residual_out[:, k * LANES:k * LANES + n] = residual[:, :n]
        feed_out[:, k * LANES:k * LANES + n] = feed[:, :n]

    for j in range(4):
        gather_x(j).wait_send()
        gather_y(j).wait_send()
        relay_a(j).wait_send()
        relay_b(j).wait_send()
        diagonal_a(j).wait_send()
        diagonal_b(j).wait_send()
        reduce_x(j).wait_send()
        reduce_y(j).wait_send()
    for j in (1, 2, 3):
        gather_z(j).wait_send()
        reduce_z(j).wait_send()
        stat_plane(j).wait_send()
        stat_z(j).wait_send()
    for copy in weight_remote:
        copy.wait_send()


def per_device(paired, stream_in, before_gain, after_gain, feed_gain, query_weight, key_weight, value_weight, output_weight, documents):
    rows, width = stream_in.shape
    full, rest = width // LANES, width % LANES
    per = LANES // rest
    size = full * rows + rows // per
    if not paired:
        query_weight, key_weight, value_weight = (
            lax.all_gather(piece, "tok", axis=0, tiled=True) for piece in (query_weight, key_weight, value_weight)
        )
        output_weight = lax.all_gather(output_weight, "tok", axis=1, tiled=True)

    def laid(gain):
        return jnp.concatenate([gain[:full * LANES], jnp.tile(gain[full * LANES:], per)])

    gains = jnp.concatenate([laid(before_gain), laid(after_gain), laid(feed_gain)]).reshape(-1, LANES)
    gains = jnp.pad(gains, ((0, 16 - gains.shape[0]), (0, 0)))
    docs = jnp.broadcast_to(documents.astype(F32)[None], (8, rows))
    tables = jnp.asarray(rope_tables())
    qcols, kcols = query_weight.shape[1], key_weight.shape[1]
    shards = 2 if paired else 1
    depth = output_weight.shape[0]
    any_spec = pl.BlockSpec(memory_space=pl.ANY)
    vmem = pl.BlockSpec(memory_space=pltpu.VMEM)
    dma = pltpu.SemaphoreType.DMA
    return pl.pallas_call(
        functools.partial(kernel, paired),
        out_shape=[jax.ShapeDtypeStruct((rows, width), BF16)] * 2,
        in_specs=[any_spec] * 8,
        out_specs=[vmem] * 2,
        scratch_shapes=[
            pltpu.VMEM((rows, width), BF16),
            pltpu.VMEM((16, size + 16, LANES), BF16),
            pltpu.VMEM((8, rows), F32),
            pltpu.VMEM((2, LENGTH, HEAD), F32),
            pltpu.VMEM((D, qcols + 2 * kcols), BF16),
            pltpu.VMEM((shards, depth, output_weight.shape[1]), BF16),
            pltpu.VMEM((16, depth, full * LANES), BF16),
            pltpu.VMEM((depth, 4 * LANES), BF16),
            pltpu.VMEM((16, size, LANES), BF16),
            pltpu.VMEM((4, size // 2, LANES), BF16),
            pltpu.VMEM((4, size // 2, LANES), BF16),
            pltpu.VMEM((4, size, LANES), BF16),
            pltpu.VMEM((4, size, LANES), BF16),
            pltpu.VMEM((3, size, LANES), BF16),
            pltpu.VMEM((8, rows), F32),
            pltpu.VMEM((3, 8, rows), F32),
            pltpu.VMEM((8, rows), F32),
            pltpu.VMEM((3, 8, rows), F32),
            dma((8,)),
            dma((4,)),
            dma((4,)),
            dma((20,)),
            dma((20,)),
            dma((19,)),
            dma((19,)),
            dma((6,)),
            dma((6,)),
        ],
        compiler_params=pltpu.CompilerParams(
            collective_id=0, has_side_effects=True, vmem_limit_bytes=56 * 1024 * 1024
        ),
    )(stream_in, gains, docs, tables, query_weight, key_weight, value_weight, output_weight)


def solution(mesh):
    both = ("hx", "hy")
    in_specs = (
        P("tok", both),
        P(both),
        P(both),
        P(both),
        P("tok", both),
        P("tok", both),
        P("tok", both),
        P(both, "tok"),
        P("tok"),
    )
    out_specs = (P("tok", both), P("tok", both))
    paired = mesh.shape["tok"] == 2
    return jax.shard_map(
        functools.partial(per_device, paired), mesh=mesh, in_specs=in_specs, out_specs=out_specs, check_vma=False
    )
```

time: 333 us -> 79.3 us (0.24)
  waiting for transfers between devices: 215 us -> 0 us
  blocking collectives: 83.7 us -> 0 us
  Pallas kernels: 0 us -> 65.9 us
  between operations: 14.2 us -> 0.65 us
  matrix products: 12 us -> 0 us
  local copies, waits for them, and re-layouts: 0.95 us -> 11.7 us
  other arithmetic: 7.35 us -> 0.68 us
    reduce_scatter x1 -> x0, waiting for transfers between devices: 130 us -> none  [per_device(): lax.psum_scatter(terms.astype(jnp.bfloat16), ('hx', 'hy'), scatter_dimens...]
    psum x2 -> x0, blocking collectives: 83.7 us -> none  [the longest x1 43.7 us: per_device(): first_sq = lax.psum(jnp.sum(wide * wide, axis=1), ('hx', 'hy'))]
    all_gather x5 -> x0, waiting for transfers between devices: 81.8 us -> none  [the longest x1 56 us: per_device(): normed = lax.all_gather(normed_local, ('hx', 'hy'), axis=1, tiled=True)]
    pallas_call x0 -> x1, Pallas kernels: none -> 65.9 us  [per_device(): pl.pallas_call(functools.partial(kernel, paired), out_shape=[jax.ShapeDty...]
    dot_general x5 -> x0, matrix products: 12 us -> none  [the longest x2 5.47 us: per_device(): jnp.dot(normed, piece, preferred_element_type=jnp.float32)]
    slice x1 -> x6, local copies, waits for them, and re-layouts: 0.02 us -> 4.1 us  [the longest x3 2.05 us: laid(): gain[full * LANES:]]
    convert_element_type x6 -> x1, other arithmetic: 4.14 us -> 0.68 us  [per_device(): docs = jnp.broadcast_to(documents.astype(F32)[None], (8, rows))]
    pallas_call x0 -> x2, local copies, waits for them, and re-layouts: none -> 3.4 us  [per_device(): pl.pallas_call(functools.partial(kernel, paired), out_shape=[jax.ShapeDty...]
  transfers between devices with their start and end apart: 6 -> 0, of which waited for: 5 -> 0; matrix products, arithmetic and copies ran while one was open for 4% -> 0% of each run, Pallas kernels for 0% -> 0%
where the time goes in v1:
time: 79.3 us; the launch traced here: 79 us
  Pallas kernels  65.9 us (83%)
  local copies, waits for them, and re-layouts  11.7 us (15%)
    pallas_call x1, Pallas kernels, per_device(): pl.pallas_call(functools.partial(kernel, paired), out_shape=[jax.ShapeDty...  65.9 us
    pallas_call x2, local copies, waits for them, and re-layouts, per_device(): pl.pallas_call(functools.partial(kernel, paired), out_shape=[jax.ShapeDty...  3.4 us
    unnamed x6, local copies, waits for them, and re-layouts  2.72 us
    slice x3, local copies, waits for them, and re-layouts, laid(): gain[full * LANES:]  2.05 us
    slice x3, local copies, waits for them, and re-layouts, laid(): gain[:full * LANES]  2.04 us

profile of v1, /device:TPU:0, one launch (start us, length us, event | category | flops | bytes accessed | tf_op | source)
XLA Modules:
  0.0 79.0 jit_solution(13010994888252246174)
XLA Ops:
  0.6 0.7 slice.19
  1.3 0.1 tile.13
  1.4 0.7 slice.18
  2.1 0.7 slice.21
  2.8 0.1 tile.30
  2.9 0.7 slice.20
  3.6 0.7 slice.23
  4.2 0.1 tile.32
  4.3 0.7 slice.22
  5.0 0.7 convert_element_type.5
  5.7 0.2 dynamic-update-slice
  5.9 0.2 dynamic-update-slice.1
  6.1 0.2 dynamic-update-slice.2
  6.3 0.2 dynamic-update-slice.3
  6.5 0.2 dynamic-update-slice.4
  6.7 0.6 pad.4.gains
  7.3 0.6 broadcast_in_dim.2.docs
  7.9 1.7 %copy.12.stream = bf16[256,288]{1,0:T(8,128)(2,1)} copy(bf16[256,288]{0,1:T(8,128)(2,1)} %param.10) | data formatting | bytes 294912 | tf_op args[0]
  9.6 65.9 %shard_map.113 = (bf16[256,288]{1,0:T(8,128)(2,1)}, bf16[256,288]{1,0:T(8,128)(2,1)}) custom-call(bf16[256,288]{1,0:T(8,128)(2,1)} %copy.12.stream, bf16[16,128]{1,0:T(8,128)(2,1)} %pad.4.gains, f32[8,256]{1,0:T(8,128)} %broadcast_in_dim.2.docs, f32[2,256,128]{2,1,0:T(8,128)} %constant.5.clone.tables, bf16[2304,256]{1,0:T(8,128)(2,1)} %wq.1, ...), custom_call_target="tpu_custom_call" | custom-call | tf_op jit(solution)/shard_map/pallas_call | solution.py:455
  75.6 1.7 %copy.13 = bf16[256,288]{0,1:T(8,128)(2,1)} copy(bf16[256,288]{1,0:T(8,128)(2,1)} %get-tuple-element.2) | data formatting | bytes 294912 | tf_op jit(solution)/shard_map/pallas_call | solution.py:455
  77.3 1.7 %copy.14 = bf16[256,288]{0,1:T(8,128)(2,1)} copy(bf16[256,288]{1,0:T(8,128)(2,1)} %get-tuple-element.3) | data formatting | bytes 294912 | tf_op jit(solution)/shard_map/pallas_call | solution.py:455
  (5 shorter events, 0.0 us)

commit v2 on v1

v2 whole, which is shorter than its diff:
```python
import functools

import jax
import jax.numpy as jnp
import numpy as np
from jax import lax
from jax.experimental import pallas as pl
from jax.experimental.pallas import tpu as pltpu
from jax.sharding import PartitionSpec as P

D = 4608
QH = 32
HEAD = 128
LENGTH = 256
LANES = 128

epsilon = 1e-06
neg_big = -1e30
MESH = pl.DeviceIdType.MESH
F32 = jnp.float32
BF16 = jnp.bfloat16


def flip(index, mask):
    low = (index % 2 + mask % 2) % 2
    high = (index // 2 + mask // 2) % 2
    return low + 2 * high


def rope_tables():
    half = HEAD // 2
    frequency = (10000.0 ** (-np.arange(half, dtype=np.float32) / half)).astype(np.float32)
    angles = frequency[:, None] * np.arange(LENGTH, dtype=np.float32)[None, :]
    return np.stack([np.cos(angles), np.sin(angles)]).astype(np.float32)


def tall_row(row):
    return jnp.broadcast_to(row, (8, row.shape[1]))


def tall(block):
    return jnp.concatenate([block] * (LANES // block.shape[0]), axis=0).T


def kernel(
    paired,
    stream, small, tables, wq, wk, wv, wo,
    residual_out, feed_out,
    slots, small_v, tables_v, weights, out_weight, out_t, acc,
    terms, first_a, first_b, from_x, from_y, from_z,
    head, head_z, head_mid, head_plane, stats, stats_in, stats_mid, stats_zin,
    local_sem, weight_send, weight_recv, gather_send, gather_recv, reduce_send, reduce_recv,
    head_send, head_recv, stat_send, stat_recv,
):
    width, rows = stream.shape
    rest = width - rows
    a, b, c = lax.axis_index("hx"), lax.axis_index("hy"), lax.axis_index("tok")
    along_x, along_y, across = flip(a, 1), flip(a, 2), flip(a, 3)
    plane = (None, along_x, along_y, across)
    z_peers = [None] + [flip(b, j) for j in (1, 2, 3)]

    def offset_of(i, j):
        return pl.multiple_of((flip(a, i) * 4 + flip(b, j)) * width, 16)

    locals_ = [
        pltpu.make_async_copy(stream, slots.at[0], local_sem.at[0]),
        pltpu.make_async_copy(small, small_v, local_sem.at[1]),
        pltpu.make_async_copy(tables, tables_v, local_sem.at[2]),
    ]
    for copy in locals_:
        copy.start()
    wrows, qcols, kcols = wq.shape[0], wq.shape[1], wk.shape[1]
    shard = c if paired else 0
    start = pl.multiple_of(shard * wrows, 16)
    targets = [
        (wq, weights.at[pl.ds(start, wrows), pl.ds(0, qcols)]),
        (wk, weights.at[pl.ds(start, wrows), pl.ds(qcols, kcols)]),
        (wv, weights.at[pl.ds(start, wrows), pl.ds(qcols + kcols, kcols)]),
        (wo, out_weight.at[shard]),
    ]
    weight_local = [
        pltpu.make_async_copy(src, dst, local_sem.at[3 + k]) for k, (src, dst) in enumerate(targets)
    ]

    barrier = pltpu.get_barrier_semaphore()
    greet = [{"hx": along_x}, {"hx": along_y}, {"hx": across}]
    greet += [{"hy": z_peers[j]} for j in (1, 2, 3)]
    if paired:
        greet.append({"tok": 1 - c})
    for peer in greet:
        pl.semaphore_signal(barrier, inc=1, device_id=peer, device_id_type=MESH)
    for copy in weight_local:
        copy.start()

    row8 = lax.broadcasted_iota(jnp.int32, (8, rows), 0)
    locals_[0].wait()
    locals_[1].wait()
    own = slots[0].astype(F32)
    small_rows = small_v[...]
    padded_tail = jnp.concatenate([small_rows[1:2, rows:rows + LANES], jnp.zeros((1, rows - LANES), F32)], axis=1)
    head[...] = jnp.where(
        row8 == 0,
        jnp.sum(own * own, axis=0, keepdims=True),
        jnp.where(row8 == 1, small_rows[1:2, :rows], jnp.where(row8 == 2, padded_tail, 0.0)),
    )
    pl.semaphore_wait(barrier, len(greet))

    def remote(src, dst, send, recv, peer):
        return pltpu.make_async_remote_copy(
            src_ref=src, dst_ref=dst, send_sem=send, recv_sem=recv, device_id=peer, device_id_type=MESH
        )

    half = width // 2
    top, bottom = pl.ds(0, half), pl.ds(half, half)

    def head_to_z(j):
        return remote(head, head_z.at[j - 1], head_send.at[j - 1], head_recv.at[j - 1], {"hy": z_peers[j]})

    def head_to_plane(i):
        return remote(head_mid, head_plane.at[i - 1], head_send.at[2 + i], head_recv.at[2 + i], {"hx": plane[i]})

    def gather_z(j):
        return remote(slots.at[0], slots.at[j], gather_send.at[j], gather_recv.at[j], {"hy": z_peers[j]})

    def gather_x(j):
        return remote(slots.at[j], slots.at[4 + j], gather_send.at[4 + j], gather_recv.at[4 + j], {"hx": along_x})

    def gather_y(j):
        return remote(slots.at[j], slots.at[8 + j], gather_send.at[8 + j], gather_recv.at[8 + j], {"hx": along_y})

    def relay_a(j):
        return remote(
            slots.at[4 + j, top], slots.at[12 + j, top], gather_send.at[12 + j], gather_recv.at[12 + j], {"hx": along_y}
        )

    def relay_b(j):
        return remote(
            slots.at[8 + j, bottom], slots.at[12 + j, bottom], gather_send.at[16 + j], gather_recv.at[16 + j], {"hx": along_x}
        )

    for j in (3, 2, 1):
        head_to_z(j).start()
    gather_x(0).start()
    gather_y(0).start()
    for j in (1, 2, 3):
        gather_z(j).start()
    weight_remote = []
    if paired:
        weight_remote = [
            remote(src, dst, weight_send.at[k], weight_recv.at[k], {"tok": 1 - c})
            for k, (src, dst) in enumerate(targets)
        ]
        for copy in weight_remote:
            copy.start()

    def forward(j):
        gather_z(j).wait_recv()
        gather_x(j).start()
        gather_y(j).start()

    def relay(j):
        gather_x(j).wait_recv()
        relay_a(j).start()
        gather_y(j).wait_recv()
        relay_b(j).start()

    for j in (1, 2, 3):
        head_to_z(j).wait_recv()
    mains = [head[...]] + [head_z[j] for j in range(3)]
    total = mains[0] + mains[1] + mains[2] + mains[3]
    tails = jnp.zeros((1, rows), F32)
    for j in range(4):
        part = mains[j][2:3, :LANES]
        if j:
            part = pltpu.roll(tall_row(part), j * rest, 1)[0:1]
        tails = tails + jnp.concatenate([part, jnp.zeros((1, rows - LANES), F32)], axis=1)
    mid = jnp.where(row8 == 0, total[0:1], 0.0)
    for j in range(4):
        mid = jnp.where(row8 == 1 + j, mains[j][1:2], mid)
    head_mid[...] = jnp.where(row8 == 5, tails, mid)
    for i in (3, 1, 2):
        head_to_plane(i).start()
    forward(1)
    relay(0)
    for i in (1, 2, 3):
        head_to_plane(i).wait_recv()
    groups = [head_mid[...]] + [head_plane[i] for i in range(3)]
    first_sq = groups[0][0:1] + groups[1][0:1] + groups[2][0:1] + groups[3][0:1]
    first_scale = lax.rsqrt(first_sq / D + epsilon)
    gain_columns = tall(jnp.concatenate(groups, axis=0))
    small_columns = tall(small_rows)
    for copy in weight_local[:3]:
        copy.wait()
    for copy in weight_remote[:3]:
        copy.wait_recv()

    def project(i, j):
        gain = jnp.concatenate(
            [gain_columns[:, 8 * i + 1 + j:8 * i + 2 + j], gain_columns[j * rest:(j + 1) * rest, 8 * i + 5:8 * i + 6]],
            axis=0,
        )
        normed = (slots[4 * i + j].astype(F32) * first_scale * gain).astype(BF16)
        part = lax.dot_general(
            weights[pl.ds(offset_of(i, j), width), :], normed, (((0,), (0,)), ((), ())), preferred_element_type=F32
        )
        if i == 0 and j == 0:
            acc[...] = part
        else:
            acc[...] += part

    shards, depth, columns = out_weight.shape

    def turn(k):
        span = 3 * LANES
        s, at = (k * span) // columns, (k * span) % columns
        out_t[k * span:(k + 1) * span, :] = out_weight[s, :, at:at + span].T

    def diagonal(j):
        relay_a(j).wait_recv()
        relay_b(j).wait_recv()
        project(3, j)

    project(0, 0)
    project(0, 1)
    forward(2)
    relay(1)
    project(0, 2)
    project(1, 0)
    project(2, 0)
    forward(3)
    relay(2)
    project(0, 3)
    project(1, 1)
    project(2, 1)
    diagonal(0)
    weight_local[3].wait()
    for copy in weight_remote[3:]:
        copy.wait_recv()
    turns = D // (3 * LANES)
    for k in range(turns // 2):
        turn(k)
    relay(3)
    project(1, 2)
    project(2, 2)
    diagonal(1)
    for k in range(turns // 2, turns):
        turn(k)
    project(1, 3)
    project(2, 3)
    locals_[2].wait()
    doc_row, doc_col = small_rows[0:1, :rows], small_columns[:rows, 0:1]
    s_index = lax.broadcasted_iota(jnp.int32, (LENGTH, LENGTH), 0)
    t_index = lax.broadcasted_iota(jnp.int32, (LENGTH, LENGTH), 1)
    diagonal(2)
    diagonal(3)

    cosine, sine = tables_v[0], tables_v[1]

    def rope(x):
        upper, lower = x[:HEAD // 2], x[HEAD // 2:]
        return jnp.concatenate([upper * cosine - lower * sine, lower * cosine + upper * sine], axis=0)

    query_heads, key_heads = qcols // HEAD, kcols // HEAD
    ratio = query_heads // key_heads
    allowed = (s_index <= t_index) & (doc_row == doc_col)
    attended = []
    for h in range(query_heads):
        kv = h // ratio
        query = (rope(acc[h * HEAD:(h + 1) * HEAD]) * (D / QH) ** (-0.5)).astype(BF16)
        key = rope(acc[qcols + kv * HEAD:qcols + (kv + 1) * HEAD]).astype(BF16)
        value = acc[qcols + kcols + kv * HEAD:qcols + kcols + (kv + 1) * HEAD].astype(BF16)
        scores = lax.dot_general(key, query, (((0,), (0,)), ((), ())), preferred_element_type=F32)
        best = jnp.max(jnp.where(allowed, scores, neg_big), axis=0, keepdims=True)
        soft = jnp.where(allowed, jnp.exp(scores - best), 0.0)
        mass = jnp.sum(soft, axis=0, keepdims=True)
        blended = jnp.dot(value, soft.astype(BF16), preferred_element_type=F32)
        attended.append((blended / mass).astype(BF16))
    attended = jnp.concatenate(attended, axis=0)

    def term(i, j):
        at = offset_of(i, j)
        terms[4 * i + j] = jnp.dot(out_t[pl.ds(at, width), :], attended, preferred_element_type=F32).astype(BF16)

    def diagonal_a(j):
        return remote(terms.at[12 + j, top], first_a.at[j], reduce_send.at[j], reduce_recv.at[j], {"hx": along_x})

    def diagonal_b(j):
        return remote(
            terms.at[12 + j, bottom], first_b.at[j], reduce_send.at[4 + j], reduce_recv.at[4 + j], {"hx": along_y}
        )

    def reduce_x(j):
        return remote(terms.at[4 + j], from_x.at[j], reduce_send.at[8 + j], reduce_recv.at[8 + j], {"hx": along_x})

    def reduce_y(j):
        return remote(terms.at[8 + j], from_y.at[j], reduce_send.at[12 + j], reduce_recv.at[12 + j], {"hx": along_y})

    def reduce_z(j):
        return remote(
            terms.at[j], from_z.at[j - 1], reduce_send.at[15 + j], reduce_recv.at[15 + j], {"hy": z_peers[j]}
        )

    def first(j):
        term(3, j)
        diagonal_a(j).start()
        diagonal_b(j).start()

    def second(j):
        term(2, j)
        term(1, j)
        diagonal_a(j).wait_recv()
        terms[8 + j, top, :] = (terms[8 + j, top, :].astype(F32) + first_a[j].astype(F32)).astype(BF16)
        reduce_y(j).start()
        diagonal_b(j).wait_recv()
        terms[4 + j, bottom, :] = (terms[4 + j, bottom, :].astype(F32) + first_b[j].astype(F32)).astype(BF16)
        reduce_x(j).start()

    def plane_sum(j):
        reduce_x(j).wait_recv()
        reduce_y(j).wait_recv()
        return terms[j].astype(F32) + from_x[j].astype(F32) + from_y[j].astype(F32)

    def third(j):
        terms[j] = plane_sum(j).astype(BF16)
        reduce_z(j).start()

    first(3)
    first(2)
    for j in (3, 2, 1, 0):
        term(0, j)
    second(3)
    first(1)
    second(2)
    first(0)
    second(1)
    third(3)
    second(0)
    third(2)
    third(1)
    mixed = plane_sum(0)
    for j in (3, 2, 1):
        reduce_z(j).wait_recv()
        mixed = mixed + from_z[j - 1].astype(F32)

    wide = slots[0].astype(F32)
    after, feed_gain = small_columns[:width, 2:3], small_columns[:width, 3:4]
    branch = mixed * after
    stats[...] = jnp.where(
        row8 == 0,
        jnp.sum(mixed * mixed, axis=0, keepdims=True),
        jnp.where(
            row8 == 1,
            jnp.sum(wide * branch, axis=0, keepdims=True),
            jnp.sum(branch * branch, axis=0, keepdims=True),
        ),
    )

    def stat_plane(i):
        return remote(stats, stats_in.at[i - 1], stat_send.at[i - 1], stat_recv.at[i - 1], {"hx": plane[i]})

    def stat_z(j):
        return remote(stats_mid, stats_zin.at[j - 1], stat_send.at[2 + j], stat_recv.at[2 + j], {"hy": z_peers[j]})

    for i in (3, 2, 1):
        stat_plane(i).start()
    for i in (1, 2, 3):
        stat_plane(i).wait_recv()
    stats_mid[...] = stats[...] + stats_in[0] + stats_in[1] + stats_in[2]
    for j in (3, 2, 1):
        stat_z(j).start()
    for j in (1, 2, 3):
        stat_z(j).wait_recv()
    summed = stats_mid[...] + stats_zin[0] + stats_zin[1] + stats_zin[2]
    after_scale = lax.rsqrt(summed[0:1] / D + epsilon)
    feed_sq = first_sq + 2.0 * after_scale * summed[1:2] + after_scale * after_scale * summed[2:3]
    feed_scale = lax.rsqrt(feed_sq / D + epsilon)
    residual = (wide + mixed * after_scale * after).astype(BF16)
    residual_out[...] = residual
    feed_out[...] = (residual.astype(F32) * feed_scale * feed_gain).astype(BF16)

    for j in range(4):
        gather_x(j).wait_send()
        gather_y(j).wait_send()
        relay_a(j).wait_send()
        relay_b(j).wait_send()
        diagonal_a(j).wait_send()
        diagonal_b(j).wait_send()
        reduce_x(j).wait_send()
        reduce_y(j).wait_send()
    for j in (1, 2, 3):
        head_to_z(j).wait_send()
        head_to_plane(j).wait_send()
        gather_z(j).wait_send()
        reduce_z(j).wait_send()
        stat_plane(j).wait_send()
        stat_z(j).wait_send()
    for copy in weight_remote:
        copy.wait_send()


def per_device(paired, stream_in, before_gain, after_gain, feed_gain, query_weight, key_weight, value_weight, output_weight, documents):
    rows, width = stream_in.shape
    if not paired:
        query_weight, key_weight, value_weight = (
            lax.all_gather(piece, "tok", axis=0, tiled=True) for piece in (query_weight, key_weight, value_weight)
        )
        output_weight = lax.all_gather(output_weight, "tok", axis=1, tiled=True)
    span = rows + LANES
    which = lax.broadcasted_iota(jnp.int32, (8, span), 0)

    def wide_row(vector):
        return jnp.pad(vector.astype(F32), (0, span - vector.shape[0]))[None]

    small = jnp.where(
        which == 0,
        wide_row(documents),
        jnp.where(
            which == 1, wide_row(before_gain), jnp.where(which == 2, wide_row(after_gain), wide_row(feed_gain))
        ),
    )
    tables = jnp.asarray(rope_tables())
    qcols, kcols = query_weight.shape[1], key_weight.shape[1]
    shards = 2 if paired else 1
    depth = output_weight.shape[0]
    any_spec = pl.BlockSpec(memory_space=pl.ANY)
    vmem = pl.BlockSpec(memory_space=pltpu.VMEM)
    dma = pltpu.SemaphoreType.DMA
    block = (width, rows)
    residual, feed_input = pl.pallas_call(
        functools.partial(kernel, paired),
        out_shape=[jax.ShapeDtypeStruct(block, BF16)] * 2,
        in_specs=[any_spec] * 7,
        out_specs=[vmem] * 2,
        scratch_shapes=[
            pltpu.VMEM((16,) + block, BF16),
            pltpu.VMEM((8, span), F32),
            pltpu.VMEM((2, HEAD // 2, LENGTH), F32),
            pltpu.VMEM((D, qcols + 2 * kcols), BF16),
            pltpu.VMEM((shards, depth, output_weight.shape[1]), BF16),
            pltpu.VMEM((D, depth), BF16),
            pltpu.VMEM((qcols + 2 * kcols, rows), F32),
            pltpu.VMEM((16,) + block, BF16),
            pltpu.VMEM((4, width // 2, rows), BF16),
            pltpu.VMEM((4, width // 2, rows), BF16),
            pltpu.VMEM((4,) + block, BF16),
            pltpu.VMEM((4,) + block, BF16),
            pltpu.VMEM((3,) + block, BF16),
        ]
        + [pltpu.VMEM((8, rows), F32), pltpu.VMEM((3, 8, rows), F32)] * 4
        + [
            dma((7,)),
            dma((4,)),
            dma((4,)),
            dma((20,)),
            dma((20,)),
            dma((19,)),
            dma((19,)),
            dma((6,)),
            dma((6,)),
            dma((6,)),
            dma((6,)),
        ],
        compiler_params=pltpu.CompilerParams(
            collective_id=0, has_side_effects=True, vmem_limit_bytes=56 * 1024 * 1024
        ),
    )(stream_in.T, small, tables, query_weight, key_weight, value_weight, output_weight)
    return residual.T, feed_input.T


def solution(mesh):
    both = ("hx", "hy")
    in_specs = (
        P("tok", both),
        P(both),
        P(both),
        P(both),
        P("tok", both),
        P("tok", both),
        P("tok", both),
        P(both, "tok"),
        P("tok"),
    )
    out_specs = (P("tok", both), P("tok", both))
    paired = mesh.shape["tok"] == 2
    return jax.shard_map(
        functools.partial(per_device, paired), mesh=mesh, in_specs=in_specs, out_specs=out_specs, check_vma=False
    )
```

time: 79.3 us -> 70.5 us (0.89)
  local copies, waits for them, and re-layouts: 11.7 us -> 3.17 us
  Pallas kernels: 65.9 us -> 63.7 us
  other arithmetic: 0.68 us -> 2.75 us
    slice x6 -> x0, local copies, waits for them, and re-layouts: 4.1 us -> none  [the longest x3 2.05 us: laid(): gain[full * LANES:]]
    pallas_call x2 -> x0, local copies, waits for them, and re-layouts: 3.4 us -> none  [per_device(): pl.pallas_call(functools.partial(kernel, paired), out_shape=[jax.ShapeDty...]
    pallas_call x1, Pallas kernels: 65.9 us -> 63.7 us  [per_device(): pl.pallas_call(functools.partial(kernel, paired), out_shape=[jax.ShapeDty...]
    pad x0 -> x2, other arithmetic: none -> 1.38 us  [wide_row(): return jnp.pad(vector.astype(F32), (0, span - vector.shape[0]))[None]]
    unnamed x6 -> x2, local copies, waits for them, and re-layouts: 2.72 us -> 3.16 us
where the time goes in v2:
time: 70.5 us; the launch traced here: 70.3 us
  Pallas kernels  63.7 us (90%)
  local copies, waits for them, and re-layouts  3.17 us (4%)
  other arithmetic  2.75 us (4%)
    pallas_call x1, Pallas kernels, per_device(): pl.pallas_call(functools.partial(kernel, paired), out_shape=[jax.ShapeDty...  63.7 us
    unnamed x2, local copies, waits for them, and re-layouts  3.16 us

profile of v2, /device:TPU:0, one launch (start us, length us, event | category | flops | bytes accessed | tf_op | source)
XLA Modules:
  0.0 70.3 jit_solution(11782873747803558144)
XLA Ops:
  0.6 0.7 convert_element_type.12
  1.3 0.7 pad_convert_fusion.2
  2.0 0.7 pad_convert_fusion
  2.7 0.7 select_select_fusion.small
  3.4 63.7 %shard_map.113 = (bf16[288,256]{1,0:T(8,128)(2,1)}, bf16[288,256]{1,0:T(8,128)(2,1)}) custom-call(bf16[288,256]{1,0:T(8,128)(2,1)} %bitcast.3, f32[8,384]{1,0:T(8,128)} %select_select_fusion.small, f32[2,64,256]{2,1,0:T(8,128)} %constant.13.clone.tables, bf16[2304,256]{1,0:T(8,128)(2,1)} %wq.1, bf16[2304,128]{1,0:T(8,128)(2,1)} %wk.1, bf16[2304,128]{1,0:T(8,128)(2,1)} %wv.1, ...), custom_call_target="tpu_custom_call" | custom-call | tf_op jit(solution)/shard_map/pallas_call | solution.py:429
  67.1 1.6 %copy.14 = bf16[256,288]{0,1:T(8,128)(2,1)} copy(bf16[256,288]{0,1:T(8,128)(2,1)} %bitcast.5) | data formatting | bytes 294912
  68.7 1.6 %copy.15 = bf16[256,288]{0,1:T(8,128)(2,1)} copy(bf16[256,288]{0,1:T(8,128)(2,1)} %bitcast.4) | data formatting | bytes 294912
  (3 shorter events, 0.0 us)

commit v3 on v2

--- a/solution.py
+++ b/solution.py
@@ -44,9 +44,9 @@
 
 def kernel(
     paired,
-    stream, small, tables, wq, wk, wv, wo,
-    residual_out, feed_out,
-    slots, small_v, tables_v, weights, out_weight, out_t, acc,
+    stream, docs, before, after_in, tables, wq, wk, wv, wo,
+    branch_out, scale_out,
+    slots, docs_v, before_v, after_v, tables_v, weights, out_weight, out_t, acc,
     terms, first_a, first_b, from_x, from_y, from_z,
     head, head_z, head_mid, head_plane, stats, stats_in, stats_mid, stats_zin,
     local_sem, weight_send, weight_recv, gather_send, gather_recv, reduce_send, reduce_recv,
@@ -64,8 +64,10 @@
 
     locals_ = [
         pltpu.make_async_copy(stream, slots.at[0], local_sem.at[0]),
-        pltpu.make_async_copy(small, small_v, local_sem.at[1]),
+        pltpu.make_async_copy(before, before_v, local_sem.at[1]),
         pltpu.make_async_copy(tables, tables_v, local_sem.at[2]),
+        pltpu.make_async_copy(docs, docs_v, local_sem.at[7]),
+        pltpu.make_async_copy(after_in, after_v, local_sem.at[8]),
     ]
     for copy in locals_:
         copy.start()
@@ -96,12 +98,16 @@
     locals_[0].wait()
     locals_[1].wait()
     own = slots[0].astype(F32)
-    small_rows = small_v[...]
-    padded_tail = jnp.concatenate([small_rows[1:2, rows:rows + LANES], jnp.zeros((1, rows - LANES), F32)], axis=1)
+    def padded(vector):
+        wide_vector = vector.astype(F32)
+        return jnp.concatenate([wide_vector, jnp.zeros((1, rows + LANES - vector.shape[1]), F32)], axis=1)
+
+    before_row = padded(before_v[...])
+    padded_tail = jnp.concatenate([before_row[:, rows:], jnp.zeros((1, rows - LANES), F32)], axis=1)
     head[...] = jnp.where(
         row8 == 0,
         jnp.sum(own * own, axis=0, keepdims=True),
-        jnp.where(row8 == 1, small_rows[1:2, :rows], jnp.where(row8 == 2, padded_tail, 0.0)),
+        jnp.where(row8 == 1, before_row[:, :rows], jnp.where(row8 == 2, padded_tail, 0.0)),
     )
     pl.semaphore_wait(barrier, len(greet))
 
@@ -119,8 +125,34 @@
     def head_to_plane(i):
         return remote(head_mid, head_plane.at[i - 1], head_send.at[2 + i], head_recv.at[2 + i], {"hx": plane[i]})
 
+    halves = (top, bottom)
+
     def gather_z(j):
         return remote(slots.at[0], slots.at[j], gather_send.at[j], gather_recv.at[j], {"hy": z_peers[j]})
+
+    def gather_z3(h):
+        part = halves[h]
+        return remote(
+            slots.at[0, part], slots.at[3, part], gather_send.at[20 + h], gather_recv.at[20 + h], {"hy": z_peers[3]}
+        )
+
+    def gather_x3(h):
+        part = halves[h]
+        return remote(
+            slots.at[3, part], slots.at[7, part], gather_send.at[22 + h], gather_recv.at[22 + h], {"hx": along_x}
+        )
+
+    def gather_y3(h):
+        part = halves[h]
+        return remote(
+            slots.at[3, part], slots.at[11, part], gather_send.at[24 + h], gather_recv.at[24 + h], {"hx": along_y}
+        )
+
+    def across_z(j, h):
+        part, k = halves[h], (13 if j == 0 else 26) + h * 2
+        return remote(
+            slots.at[12 + j, part], slots.at[13 + j, part], gather_send.at[k], gather_recv.at[k], {"hy": z_peers[1]}
+        )
 
     def gather_x(j):
         return remote(slots.at[j], slots.at[4 + j], gather_send.at[4 + j], gather_recv.at[4 + j], {"hx": along_x})
@@ -142,8 +174,10 @@
         head_to_z(j).start()
     gather_x(0).start()
     gather_y(0).start()
-    for j in (1, 2, 3):
+    for j in (1, 2):
         gather_z(j).start()
+    gather_z3(0).start()
+    gather_z3(1).start()
     weight_remote = []
     if paired:
         weight_remote = [
@@ -163,6 +197,12 @@
         relay_a(j).start()
         gather_y(j).wait_recv()
         relay_b(j).start()
+
+    def spread(j):
+        relay_a(j).wait_recv()
+        across_z(j, 0).start()
+        relay_b(j).wait_recv()
+        across_z(j, 1).start()
 
     for j in (1, 2, 3):
         head_to_z(j).wait_recv()
@@ -188,7 +228,6 @@
     first_sq = groups[0][0:1] + groups[1][0:1] + groups[2][0:1] + groups[3][0:1]
     first_scale = lax.rsqrt(first_sq / D + epsilon)
     gain_columns = tall(jnp.concatenate(groups, axis=0))
-    small_columns = tall(small_rows)
     for copy in weight_local[:3]:
         copy.wait()
     for copy in weight_remote[:3]:
@@ -215,44 +254,54 @@
         s, at = (k * span) // columns, (k * span) % columns
         out_t[k * span:(k + 1) * span, :] = out_weight[s, :, at:at + span].T
 
-    def diagonal(j):
-        relay_a(j).wait_recv()
-        relay_b(j).wait_recv()
-        project(3, j)
-
     project(0, 0)
     project(0, 1)
     forward(2)
-    relay(1)
+    spread(0)
     project(0, 2)
+    gather_x(1).wait_recv()
+    gather_y(1).wait_recv()
     project(1, 0)
     project(2, 0)
-    forward(3)
     relay(2)
+    for h in range(2):
+        gather_z3(h).wait_recv()
+        gather_x3(h).start()
+        gather_y3(h).start()
     project(0, 3)
     project(1, 1)
     project(2, 1)
-    diagonal(0)
+    project(3, 0)
+    spread(2)
     weight_local[3].wait()
     for copy in weight_remote[3:]:
         copy.wait_recv()
     turns = D // (3 * LANES)
-    for k in range(turns // 2):
+    for k in range(turns):
         turn(k)
-    relay(3)
     project(1, 2)
     project(2, 2)
-    diagonal(1)
-    for k in range(turns // 2, turns):
-        turn(k)
+    across_z(0, 0).wait_recv()
+    across_z(0, 1).wait_recv()
+    project(3, 1)
+    project(3, 2)
+    locals_[2].wait()
+    locals_[3].wait()
+    locals_[4].wait()
+    doc_row = docs_v[...].astype(F32)
+    after_row = padded(after_v[...])
+    doc_col = tall(jnp.broadcast_to(doc_row, (8, rows)))[:, 0:1]
+    after = tall(jnp.broadcast_to(after_row, (8, rows + LANES)))[:width, 0:1]
+    s_index = lax.broadcasted_iota(jnp.int32, (LENGTH, LENGTH), 0)
+    t_index = lax.broadcasted_iota(jnp.int32, (LENGTH, LENGTH), 1)
+    for h in range(2):
+        gather_x3(h).wait_recv()
+        gather_y3(h).wait_recv()
     project(1, 3)
     project(2, 3)
-    locals_[2].wait()
-    doc_row, doc_col = small_rows[0:1, :rows], small_columns[:rows, 0:1]
-    s_index = lax.broadcasted_iota(jnp.int32, (LENGTH, LENGTH), 0)
-    t_index = lax.broadcasted_iota(jnp.int32, (LENGTH, LENGTH), 1)
-    diagonal(2)
-    diagonal(3)
+    across_z(2, 0).wait_recv()
+    across_z(2, 1).wait_recv()
+    project(3, 3)
 
     cosine, sine = tables_v[0], tables_v[1]
 
@@ -300,6 +349,24 @@
             terms.at[j], from_z.at[j - 1], reduce_send.at[15 + j], reduce_recv.at[15 + j], {"hy": z_peers[j]}
         )
 
+    def last_x(h):
+        part = halves[h]
+        return remote(
+            terms.at[5, part], from_x.at[1, part], reduce_send.at[19 + h], reduce_recv.at[19 + h], {"hx": along_x}
+        )
+
+    def last_y(h):
+        part = halves[h]
+        return remote(
+            terms.at[9, part], from_y.at[1, part], reduce_send.at[21 + h], reduce_recv.at[21 + h], {"hx": along_y}
+        )
+
+    def last_z(h):
+        part = halves[h]
+        return remote(
+            terms.at[1, part], from_z.at[0, part], reduce_send.at[23 + h], reduce_recv.at[23 + h], {"hy": z_peers[1]}
+        )
+
     def first(j):
         term(3, j)
         diagonal_a(j).start()
@@ -310,10 +377,18 @@
         term(1, j)
         diagonal_a(j).wait_recv()
         terms[8 + j, top, :] = (terms[8 + j, top, :].astype(F32) + first_a[j].astype(F32)).astype(BF16)
-        reduce_y(j).start()
+        if j == 1:
+            last_y(0).start()
+            last_y(1).start()
+        else:
+            reduce_y(j).start()
         diagonal_b(j).wait_recv()
         terms[4 + j, bottom, :] = (terms[4 + j, bottom, :].astype(F32) + first_b[j].astype(F32)).astype(BF16)
-        reduce_x(j).start()
+        if j == 1:
+            last_x(0).start()
+            last_x(1).start()
+        else:
+            reduce_x(j).start()
 
     def plane_sum(j):
         reduce_x(j).wait_recv()
@@ -336,14 +411,23 @@
     third(3)
     second(0)
     third(2)
-    third(1)
+    for h in range(2):
+        last_x(h).wait_recv()
+        last_y(h).wait_recv()
+        part = halves[h]
+        summed = terms[1, part, :].astype(F32) + from_x[1, part, :].astype(F32) + from_y[1, part, :].astype(F32)
+        terms[1, part, :] = summed.astype(BF16)
+        last_z(h).start()
     mixed = plane_sum(0)
     for j in (3, 2, 1):
-        reduce_z(j).wait_recv()
+        if j == 1:
+            last_z(0).wait_recv()
+            last_z(1).wait_recv()
+        else:
+            reduce_z(j).wait_recv()
         mixed = mixed + from_z[j - 1].astype(F32)
 
     wide = slots[0].astype(F32)
-    after, feed_gain = small_columns[:width, 2:3], small_columns[:width, 3:4]
     branch = mixed * after
     stats[...] = jnp.where(
         row8 == 0,
@@ -374,26 +458,35 @@
     after_scale = lax.rsqrt(summed[0:1] / D + epsilon)
     feed_sq = first_sq + 2.0 * after_scale * summed[1:2] + after_scale * after_scale * summed[2:3]
     feed_scale = lax.rsqrt(feed_sq / D + epsilon)
-    residual = (wide + mixed * after_scale * after).astype(BF16)
-    residual_out[...] = residual
-    feed_out[...] = (residual.astype(F32) * feed_scale * feed_gain).astype(BF16)
+    branch_out[...] = branch
+    scale_out[...] = jnp.where(row8 == 0, after_scale, feed_scale)
 
     for j in range(4):
-        gather_x(j).wait_send()
-        gather_y(j).wait_send()
+        if j < 3:
+            gather_x(j).wait_send()
+            gather_y(j).wait_send()
+        diagonal_a(j).wait_send()
+        diagonal_b(j).wait_send()
+        if j != 1:
+            reduce_x(j).wait_send()
+            reduce_y(j).wait_send()
+    for j in (0, 2):
         relay_a(j).wait_send()
         relay_b(j).wait_send()
-        diagonal_a(j).wait_send()
-        diagonal_b(j).wait_send()
-        reduce_x(j).wait_send()
-        reduce_y(j).wait_send()
+    for h in range(2):
+        for copy in (gather_z3, gather_x3, gather_y3, last_x, last_y, last_z):
+            copy(h).wait_send()
+        across_z(0, h).wait_send()
+        across_z(2, h).wait_send()
     for j in (1, 2, 3):
         head_to_z(j).wait_send()
         head_to_plane(j).wait_send()
-        gather_z(j).wait_send()
-        reduce_z(j).wait_send()
         stat_plane(j).wait_send()
         stat_z(j).wait_send()
+    for j in (1, 2):
+        gather_z(j).wait_send()
+    for j in (2, 3):
+        reduce_z(j).wait_send()
     for copy in weight_remote:
         copy.wait_send()
 
@@ -405,19 +498,6 @@
             lax.all_gather(piece, "tok", axis=0, tiled=True) for piece in (query_weight, key_weight, value_weight)
         )
         output_weight = lax.all_gather(output_weight, "tok", axis=1, tiled=True)
-    span = rows + LANES
-    which = lax.broadcasted_iota(jnp.int32, (8, span), 0)
-
-    def wide_row(vector):
-        return jnp.pad(vector.astype(F32), (0, span - vector.shape[0]))[None]
-
-    small = jnp.where(
-        which == 0,
-        wide_row(documents),
-        jnp.where(
-            which == 1, wide_row(before_gain), jnp.where(which == 2, wide_row(after_gain), wide_row(feed_gain))
-        ),
-    )
     tables = jnp.asarray(rope_tables())
     qcols, kcols = query_weight.shape[1], key_weight.shape[1]
     shards = 2 if paired else 1
@@ -426,14 +506,16 @@
     vmem = pl.BlockSpec(memory_space=pltpu.VMEM)
     dma = pltpu.SemaphoreType.DMA
     block = (width, rows)
-    residual, feed_input = pl.pallas_call(
+    branch, scales = pl.pallas_call(
         functools.partial(kernel, paired),
-        out_shape=[jax.ShapeDtypeStruct(block, BF16)] * 2,
-        in_specs=[any_spec] * 7,
+        out_shape=[jax.ShapeDtypeStruct(block, F32), jax.ShapeDtypeStruct((8, rows), F32)],
+        in_specs=[any_spec] * 9,
         out_specs=[vmem] * 2,
         scratch_shapes=[
             pltpu.VMEM((16,) + block, BF16),
-            pltpu.VMEM((8, span), F32),
+            pltpu.VMEM((1, rows), jnp.int32),
+            pltpu.VMEM((1, width), BF16),
+            pltpu.VMEM((1, width), BF16),
             pltpu.VMEM((2, HEAD // 2, LENGTH), F32),
             pltpu.VMEM((D, qcols + 2 * kcols), BF16),
             pltpu.VMEM((shards, depth, output_weight.shape[1]), BF16),
@@ -448,13 +530,13 @@
         ]
         + [pltpu.VMEM((8, rows), F32), pltpu.VMEM((3, 8, rows), F32)] * 4
         + [
-            dma((7,)),
+            dma((9,)),
             dma((4,)),
             dma((4,)),
-            dma((20,)),
-            dma((20,)),
-            dma((19,)),
-            dma((19,)),
+            dma((29,)),
+            dma((29,)),
+            dma((25,)),
+            dma((25,)),
             dma((6,)),
             dma((6,)),
             dma((6,)),
@@ -463,8 +545,22 @@
         compiler_params=pltpu.CompilerParams(
             collective_id=0, has_side_effects=True, vmem_limit_bytes=56 * 1024 * 1024
         ),
-    )(stream_in.T, small, tables, query_weight, key_weight, value_weight, output_weight)
-    return residual.T, feed_input.T
+    )(
+        stream_in.T,
+        documents.reshape(1, rows),
+        before_gain.reshape(1, width),
+        after_gain.reshape(1, width),
+        tables,
+        query_weight,
+        key_weight,
+        value_weight,
+        output_weight,
+    )
+    after_scale, feed_scale = scales[0][:, None], scales[1][:, None]
+    wide = stream_in.astype(F32)
+    residual = (wide + branch.T * after_scale).astype(BF16)
+    feed_input = (residual.astype(F32) * feed_scale * feed_gain.astype(F32)[None, :]).astype(BF16)
+    return residual, feed_input
 
 
 def solution(mesh):

time: 70.5 us -> 70 us (level)
    unnamed x2, local copies, waits for them, and re-layouts: 3.16 us -> 0.01 us
    reshape x0 -> x2, local copies, waits for them, and re-layouts: none -> 2.49 us  [the longest x1 1.24 us: per_device(): before_gain.reshape(1, width)]
    convert_element_type x1 -> x2, other arithmetic: 0.68 us -> 2.41 us  [the longest x1 1.73 us: per_device(): (residual.astype(F32) * feed_scale * feed_gain.astype(F32)[None, :]).asty...]
    pad x2 -> x0, other arithmetic: 1.38 us -> none  [wide_row(): return jnp.pad(vector.astype(F32), (0, span - vector.shape[0]))[None]]
    slice x0 -> x1, local copies, waits for them, and re-layouts: none -> 0.78 us  [per_device(): after_scale, feed_scale = (scales[0][:, None], scales[1][:, None])]
where the time goes in v3:
time: 70 us; the launch traced here: 69.7 us
  Pallas kernels  63.4 us (91%)
  local copies, waits for them, and re-layouts  3.27 us (5%)
  other arithmetic  2.41 us (3%)
    pallas_call x1, Pallas kernels, per_device(): pl.pallas_call(functools.partial(kernel, paired), out_shape=[jax.ShapeDty...  63.4 us
    convert_element_type x1, other arithmetic, per_device(): (residual.astype(F32) * feed_scale * feed_gain.astype(F32)[None, :]).asty...  1.73 us

profile of v3, /device:TPU:0, one launch (start us, length us, event | category | flops | bytes accessed | tf_op | source)
XLA Modules:
  0.0 69.7 jit_solution(9755306559536062955)
XLA Ops:
  0.6 1.2 %reshape.17.before = bf16[1,288]{1,0:T(2,128)(2,1)} reshape(bf16[288]{0:T(512)(128)(2,1)} %param.11) | data formatting | bytes 1152 | tf_op jit(solution)/shard_map/reshape | solution.py:551
  1.9 1.2 %reshape.18.after_in = bf16[1,288]{1,0:T(2,128)(2,1)} reshape(bf16[288]{0:T(512)(128)(2,1)} %param.12) | data formatting | bytes 1152 | tf_op jit(solution)/shard_map/reshape | solution.py:552
  3.1 0.7 convert_element_type.18
  3.8 0.0 copy-start
  3.8 63.4 %shard_map.113 = (f32[288,256]{1,0:T(8,128)}, f32[8,256]{1,0:T(8,128)}) custom-call(bf16[288,256]{1,0:T(8,128)(2,1)} %bitcast.9, s32[1,256]{1,0:T(1,128)} %bitcast.12, bf16[1,288]{1,0:T(2,128)(2,1)} %reshape.17.before, bf16[1,288]{1,0:T(2,128)(2,1)} %reshape.18.after_in, f32[2,64,256]{2,1,0:T(8,128)} %constant.2.clone.tables, bf16[2304,256]{1,0:T(8,128)(2,1)} %wq.1, ...), custom_call_target="tpu_custom_call" | custom-call | tf_op jit(solution)/shard_map/pallas_call | solution.py:509
  67.2 0.8 %fusion.2 = (f32[1,256]{1,0:T(1,128)S(1)}, f32[1,256]{1,0:T(1,128)S(1)}) fusion(f32[8,256]{1,0:T(8,128)} %get-tuple-element.5), kind=kLoop, calls=%fused_computation.3 | loop fusion | bytes 4096 | tf_op jit(solution)/shard_map/slice | solution.py:559
  68.0 0.0 copy-done
  68.0 1.7 %multiply_convert_fusion = (bf16[256,288]{0,1:T(8,128)(2,1)}, bf16[256,288]{0,1:T(8,128)(2,1)}) fusion(f32[288]{0:T(512)S(1)} %convert_element_type.18, f32[256]{0:T(256)S(1)} %bitcast.11, f32[288,256]{1,0:T(8,128)} %get-tuple-element.4, f32[256]{0:T(256)S(1)} %bitcast.10, bf16[256,288]{0,1:T(8,128)(2,1)S(1)} %copy-done), kind=kLoop, calls=%fused_computation.2 | loop fusion | flops 589824 | bytes 740480 | tf_op jit(solution)/shard_map/convert_element_type | solution.py:562
Async XLA Ops:
  3.8 64.2 %copy-start = (bf16[256,288]{0,1:T(8,128)(2,1)S(1)}, bf16[256,288]{0,1:T(8,128)(2,1)}, u32[]{:S(2)}) copy-start(bf16[256,288]{0,1:T(8,128)(2,1)} %param.10) | copy-start | bytes 442372
